TPU v7x, 512 devices: a 4x2x32 block of a 4x8x32 slice. The times are simulated.
512 devices in a mesh: grp: 2 (over y), gy: 32 (over z), gx: 4 (over x), gz: 2 (over core).
Axes of the slice: x: 4, y: 2, z: 32, core: 2. Of those that a mesh axis runs over, the one named last changes fastest.
The devices are a block of a 4x8x32 slice.
Arguments:
- pair: bfloat16 [1024, 512, 128], P(('grp', 'gx', 'gz'), 'gy'), parts along dimension 0, may hold values from -6 to 6
- lengths: int32 [2], P('grp'), parts along dimension 0, may hold values from 256 to 512
- ln_gain: float32 [128], replicated, may hold values from 0.1 to 1.9
- ln_bias: float32 [128], replicated, may hold values from -3 to 3
- w_ab: bfloat16 [128, 512], replicated, may hold values from -0.5 to 0.5
- w_gate: bfloat16 [128, 128], replicated, may hold values from -0.5 to 0.5
- out_gain: float32 [128], replicated, may hold values from 0.1 to 1.9
- out_bias: float32 [128], replicated, may hold values from -3 to 3
- w_out: bfloat16 [128, 128], replicated, may hold values from -0.5 to 0.5
Outputs:
- update: bfloat16 [1024, 512, 128], P(('grp', 'gx', 'gz'), 'gy'), parts along dimension 0
There are 2 independent parts, one for each index of `grp`. A program takes and returns all parts, laid end to end along the dimension named above; an argument that names none is the same for every part. Nothing has to cross between parts.
Inputs may be any that keep to these rules, and one draw needn't show every extreme that they name: Residues from lengths[0] on are padding.
All inputs are finite; a program needn't handle non-finite values.
Results may differ from a plain program's by a relative error of at most 0.0052.
Values may be sent and summed in bfloat16 or wider, within the bound.
A program may use at most 128 MiB of HBM per device.

v0:
```python
import jax
import jax.numpy as jnp
from jax import lax
from jax.sharding import PartitionSpec as P


def from_everyone(value, axis):
    copies = jnp.broadcast_to(value, (lax.axis_size(axis), *value.shape))
    return lax.all_to_all(copies, axis, split_axis=0, concat_axis=0, tiled=True)


def in_order(tiles, dim):
    shape = list(tiles.shape[1:])
    shape[dim] *= tiles.shape[0]
    return jnp.moveaxis(tiles, 0, dim).reshape(shape)


def collect(value, axis, dim):
    tiles = from_everyone(value, axis)
    return in_order(tiles, dim)


def layer_norm(values, gain, bias):
    values = values.astype(jnp.float32)
    mean = jnp.mean(values, -1, keepdims=True)
    spread = jnp.mean(jnp.square(values - mean), -1, keepdims=True)
    return (values - mean) * lax.rsqrt(spread + 1e-05) * gain + bias


def channel_norm(values, gain, bias):
    mean = jnp.mean(values, 0, keepdims=True)
    spread = jnp.mean(jnp.square(values - mean), 0, keepdims=True)
    return (values - mean) * lax.rsqrt(spread + 1e-05) * gain[:, None, None] + bias[:, None, None]


def body(pair, lengths, ln_gain, ln_bias, w_ab, w_gate, out_gain, out_bias, w_out):
    tile_rows, tile_cols, width = pair.shape
    hidden = w_out.shape[0]
    row_start = lax.axis_index(("gx", "gz")) * tile_rows
    col_index = lax.axis_index("gy")
    col_start = col_index * tile_cols
    normed = layer_norm(pair, ln_gain, ln_bias).astype(jnp.bfloat16)
    flat = normed.reshape(tile_rows * tile_cols, width)
    proj = jnp.dot(flat, w_ab, preferred_element_type=jnp.float32).reshape(
        tile_rows, tile_cols, 4 * hidden
    )
    row_live = (row_start + jnp.arange(tile_rows, dtype=jnp.int32) < lengths[0]).astype(jnp.float32)
    col_live = (col_start + jnp.arange(tile_cols, dtype=jnp.int32) < lengths[0]).astype(jnp.float32)
    pair_mask = (row_live[:, None] * col_live[None, :])[..., None]
    left = (pair_mask * jax.nn.sigmoid(proj[..., :hidden]) * proj[..., hidden : 2 * hidden]).astype(
        jnp.bfloat16
    )
    right = (
        pair_mask * jax.nn.sigmoid(proj[..., 2 * hidden : 3 * hidden]) * proj[..., 3 * hidden :]
    ).astype(jnp.bfloat16)
    left_major = jnp.transpose(left, (2, 0, 1))
    right_major = jnp.transpose(right, (2, 0, 1))
    column_rows = collect(right_major, ("gx", "gz"), 1)
    right_mine = lax.all_to_all(column_rows, "gy", split_axis=1, concat_axis=2, tiled=True)
    triangle = jnp.einsum(
        "cik,cjk->cij",
        lax.all_gather(left_major, "gy", axis=2, tiled=True),
        right_mine,
        preferred_element_type=jnp.float32,
    )
    tri_norm = channel_norm(triangle, out_gain, out_bias).astype(jnp.bfloat16)
    gate = jax.nn.sigmoid(jnp.dot(flat, w_gate, preferred_element_type=jnp.float32)).reshape(
        tile_rows, tile_cols, width
    )
    projected = jnp.einsum("cij,cd->ijd", tri_norm, w_out, preferred_element_type=jnp.float32)
    return (gate * projected).astype(jnp.bfloat16)


def solution(mesh):
    in_specs = (P(("grp", "gx", "gz"), "gy", None), P("grp"), P(), P(), P(), P(), P(), P(), P())
    out_specs = P(("grp", "gx", "gz"), "gy", None)
    return jax.shard_map(body, mesh=mesh, in_specs=in_specs, out_specs=out_specs, check_vma=False)
```

profile of v0, /device:TPU:36, one launch (start us, length us, event | category | flops | bytes accessed | tf_op | source)
XLA Modules:
  0.0 454.5 jit_solution(10846532416130291619)
XLA Ops:
  6.5 0.0 copy-start
  7.2 1.2 convert_reduce_fusion
  8.4 0.1 copy.35
  8.5 0.1 copy.36
  8.6 1.3 fusion.6
  9.9 0.1 copy.37
  10.0 0.1 copy.38
  10.1 0.1 broadcast_multiply_fusion
  10.2 1.3 fusion.9
  11.5 0.0 copy-done
  11.5 0.4 fusion.22
  11.9 1.0 fusion.21
  12.9 1.6 broadcast_in_dim.2
  14.5 44.6 %all-to-all-start = ((bf16[8,128,64,16]{1,3,2,0:T(8,128)(2,1)}), bf16[8,128,64,16]{1,3,2,0:T(8,128)(2,1)}, u32[]{:S(2)}, u32[]{:S(2)}) async-start(bf16[8,128,64,16]{1,3,2,0:T(8,128)(2,1)} %broadcast_in_dim.2), calls=%async_computation | async-start | bytes 4194304 | tf_op jit(solution)/shard_map/all_to_all | solution.py:9
  59.1 0.0 all-gather.2.cloned.1.call-start
  59.1 0.7 all-gather.2.cloned.1.call-update
  59.8 23.3 %all-to-all-done = bf16[8,128,64,16]{1,3,2,0:T(8,128)(2,1)} async-done(((bf16[8,128,64,16]{1,3,2,0:T(8,128)(2,1)}), bf16[8,128,64,16]{1,3,2,0:T(8,128)(2,1)}, u32[]{:S(2)}, u32[]{:S(2)}) %all-to-all-start) | async-done | bytes 2097184 | tf_op jit(solution)/shard_map/all_to_all | solution.py:9
  83.2 0.0 copy-start.4
  83.2 6.2 %all-to-all-start.1 = ((bf16[128,512,16]{0,2,1:T(8,128)(2,1)}), bf16[128,512,16]{0,2,1:T(8,128)(2,1)S(1)}, u32[]{:S(2)}, u32[]{:S(2)}) async-start(bf16[128,512,16]{0,2,1:T(8,128)(2,1)} %bitcast.7), calls=%async_computation.1 | async-start | bytes 4194304 | tf_op jit(solution)/shard_map/all_to_all | solution.py:59
  89.4 0.0 copy-done.4
  89.4 0.3 fusion.2
  89.7 314.3 %all-gather.2.cloned.1.call-done = bf16[128,64,512]{0,2,1:T(8,128)(2,1)} async-done(((bf16[128,64,16]{0,2,1:T(8,128)(2,1)}), bf16[128,64,512]{0,2,1:T(8,128)(2,1)}) %all-gather.2.cloned.1.call-update) | async-done | bytes 8388624 | tf_op jit(solution)/shard_map/all_gather | solution.py:62
  404.0 29.2 %copy.40 = bf16[128,64,512]{1,2,0:T(8,128)(2,1)} copy(bf16[128,64,512]{0,2,1:T(8,128)(2,1)} %all-gather.2.cloned.1.call-done) | data formatting | bytes 16777216 | tf_op jit(solution)/shard_map/all_gather | solution.py:62
  433.2 0.0 all-to-all-done.1
  433.2 1.9 copy.39
  435.0 3.4 copy.41
  438.5 0.0 copy-start.2
  438.5 0.0 copy-start.3
  438.5 7.1 %fusion.25 = (f32[64,16]{0,1:T(8,128)S(1)}, f32[128,64,16]{1,2,0:T(8,128)S(1)}) fusion(bf16[128,16,512]{2,1,0:T(8,128)(2,1)S(1)} %copy.41, bf16[128,64,512]{1,2,0:T(8,128)(2,1)} %copy.40), kind=kOutput, calls=%fused_computation.42 | convolution fusion | flops 134347776 | bytes 11014144 | tf_op jit(solution)/shard_map/cik,cjk->cij/dot_general | solution.py:60
  445.6 0.0 copy-start.1
  445.6 0.2 multiply_reduce_fusion
  445.8 0.0 copy-done.2
  445.8 0.0 copy-done.3
  445.8 0.3 add_convert_fusion
  446.2 0.6 copy.42
  446.8 0.0 copy-done.1
  446.8 0.9 fusion.3
  (6 shorter events, 0.0 us)
Async XLA Ops:
  6.5 4.9 %copy-start = (bf16[128,512]{1,0:T(8,128)(2,1)S(1)}, bf16[128,512]{1,0:T(8,128)(2,1)}, u32[]{:S(2)}) copy-start(bf16[128,512]{1,0:T(8,128)(2,1)} %param.13) | copy-start | bytes 393220
  14.5 68.6 %all-to-all-start = ((bf16[8,128,64,16]{1,3,2,0:T(8,128)(2,1)}), bf16[8,128,64,16]{1,3,2,0:T(8,128)(2,1)}, u32[]{:S(2)}, u32[]{:S(2)}) async-start(bf16[8,128,64,16]{1,3,2,0:T(8,128)(2,1)} %broadcast_in_dim.2), calls=%async_computation | async-start | bytes 4194304 | tf_op jit(solution)/shard_map/all_to_all | solution.py:9
  59.1 344.9 %all-gather.2.cloned.1.call-start = ((), (), s32[]{:S(2)}) async-start(), calls=%async_computation.2 | async-start | bytes 8650752 | tf_op jit(solution)/shard_map/all_gather | solution.py:62
  83.2 6.2 %copy-start.4 = (bf16[128,128]{1,0:T(8,128)(2,1)S(1)}, bf16[128,128]{1,0:T(8,128)(2,1)}, u32[]{:S(2)}) copy-start(bf16[128,128]{1,0:T(8,128)(2,1)} %param.14) | copy-start | bytes 98308
  83.2 350.0 %all-to-all-start.1 = ((bf16[128,512,16]{0,2,1:T(8,128)(2,1)}), bf16[128,512,16]{0,2,1:T(8,128)(2,1)S(1)}, u32[]{:S(2)}, u32[]{:S(2)}) async-start(bf16[128,512,16]{0,2,1:T(8,128)(2,1)} %bitcast.7), calls=%async_computation.1 | async-start | bytes 4194304 | tf_op jit(solution)/shard_map/all_to_all | solution.py:59
  438.5 7.3 %copy-start.2 = (f32[128]{0:T(128)S(1)}, f32[128]{0:T(128)}, u32[]{:S(2)}) copy-start(f32[128]{0:T(128)} %param.16) | copy-start | bytes 1540
  438.5 7.3 %copy-start.3 = (f32[128]{0:T(128)S(1)}, f32[128]{0:T(128)}, u32[]{:S(2)}) copy-start(f32[128]{0:T(128)} %param.15) | copy-start | bytes 1540
  445.6 1.2 copy-start.1
Sparse Core Ops, SparseCore 0:
  61.9 342.0 all-gather.1
where the time goes:
time: 455 us
  waiting for transfers between devices  338 us (74%)
  starting transfers between devices  50.8 us (11%)
  local copies, waits for them, and re-layouts  37 us (8%)
  between operations  14.3 us (3%)
  matrix products  8.67 us (2%)
  other arithmetic  5.46 us (1%)
    all_gather x1, waiting for transfers between devices, body(): lax.all_gather(left_major, 'gy', axis=2, tiled=True)  314 us
    all_to_all x1, starting transfers between devices, from_everyone(): return lax.all_to_all(copies, axis, split_axis=0, concat_axis=0, tiled=True)  44.6 us
    all_gather x1, local copies, waits for them, and re-layouts, body(): lax.all_gather(left_major, 'gy', axis=2, tiled=True)  29.2 us
    all_to_all x1, waiting for transfers between devices, from_everyone(): return lax.all_to_all(copies, axis, split_axis=0, concat_axis=0, tiled=True)  23.3 us
  transfers between devices with their start and end apart: 3, of which 2 were waited for; matrix products, arithmetic and copies ran while one was open for 6% of the time, Pallas kernels for 0%

commit v1 on v0

v1 whole, which is shorter than its diff:
```python
import functools

import jax
import jax.numpy as jnp
from jax import lax
from jax.experimental import pallas as pl
from jax.experimental.pallas import tpu as pltpu
from jax.sharding import PartitionSpec as P

MESH = pl.DeviceIdType.MESH
F32 = jnp.float32
BF16 = jnp.bfloat16


def kernel(
    dims,
    pair_ref,
    len_ref,
    ln_gain_ref,
    ln_bias_ref,
    w_ab_ref,
    w_gate_ref,
    out_gain_ref,
    out_bias_ref,
    w_out_ref,
    out_ref,
    norm_f32,
    buf_l,
    buf_r,
    gate_buf,
    send_l,
    send_r,
    recv_l,
    all_r,
    send_t,
    recv_t,
    y_buf,
    o_buf,
    wo_buf,
    gm_buf,
    bm_buf,
    send_sem,
    recv_sem,
):
    nz, nx, ng, rows, cols = dims
    nd = nx * ng
    z = lax.axis_index("gy")
    x = lax.axis_index("gx")
    g = lax.axis_index("gz")
    d_me = x * ng + g
    length = len_ref[0]
    half = 64

    barrier = pltpu.get_barrier_semaphore()
    for j in range(1, nz):
        pl.semaphore_signal(
            barrier, inc=1, device_id={"gy": lax.rem(z + j, nz)}, device_id_type=MESH
        )
    for j in range(1, nd):
        peer = lax.rem(d_me + j, nd)
        pl.semaphore_signal(
            barrier,
            inc=1,
            device_id={"gx": peer // ng, "gz": lax.rem(peer, ng)},
            device_id_type=MESH,
        )

    xs = pair_ref[...].astype(F32)
    mean = jnp.mean(xs, -1, keepdims=True)
    cen = xs - mean
    var = jnp.mean(cen * cen, -1, keepdims=True)
    normed = (cen * lax.rsqrt(var + 1e-05) * ln_gain_ref[...] + ln_bias_ref[...]).astype(BF16)
    norm_f32[...] = normed.astype(F32)
    gate_buf[...] = jax.nn.sigmoid(jnp.dot(normed, w_gate_ref[...], preferred_element_type=F32))

    w_t = w_ab_ref[...].T
    lane = lax.broadcasted_iota(jnp.int32, (1, 128), 1)
    lane_i = lax.rem(lane, half)
    lane_h = lane // half
    i_live = (d_me * rows + lane_i) < length
    for t in range(cols // 2):
        n_t = jnp.concatenate(
            [
                norm_f32[pl.ds(2 * t, rows, stride=cols), :],
                norm_f32[pl.ds(2 * t + 1, rows, stride=cols), :],
            ],
            axis=0,
        ).astype(BF16)
        proj = lax.dot_general(
            w_t, n_t, (((1,), (1,)), ((), ())), preferred_element_type=F32
        )
        k_live = (z * cols + 2 * t + lane_h) < length
        mask = jnp.where(jnp.logical_and(i_live, k_live), 1.0, 0.0)
        buf_l[pl.ds(t, 128, stride=8), :] = mask * jax.nn.sigmoid(proj[0:128]) * proj[128:256]
        buf_r[pl.ds(t, 128, stride=8), :] = mask * jax.nn.sigmoid(proj[256:384]) * proj[384:512]
    send_r[...] = buf_r[...].astype(BF16).reshape(send_r.shape)
    send_l[...] = buf_l[...].astype(BF16).reshape(send_l.shape)
    recv_l[z] = send_l[z]
    all_r[d_me, z] = send_r[z]

    pl.semaphore_wait(barrier, nz - 1 + nd - 1)

    offsets = []
    for j in range(nz // 2, 0, -1):
        offsets.append(j)
        if 2 * j != nz:
            offsets.append(nz - j)

    def to_z(src, dst, k, target):
        return pltpu.make_async_remote_copy(
            src, dst, send_sem.at[k], recv_sem.at[k], device_id={"gy": target}, device_id_type=MESH
        )

    for j in offsets:
        target = lax.rem(z + j, nz)
        to_z(send_r.at[target], all_r.at[d_me, z], 0, target).start()
    for j in offsets:
        target = lax.rem(z + j, nz)
        to_z(send_l.at[target], recv_l.at[z], 1, target).start()

    wo_buf[...] = w_out_ref[...].astype(F32)
    w2 = jnp.concatenate(
        [wo_buf[pl.ds(0, 64, stride=2), :], wo_buf[pl.ds(1, 64, stride=2), :]], axis=1
    ).astype(BF16)
    row_m = lax.broadcasted_iota(jnp.int32, (64, 128), 0)
    lane_c = lax.broadcasted_iota(jnp.int32, (64, 128), 1)
    for src, dst in ((out_gain_ref, gm_buf), (out_bias_ref, bm_buf)):
        vals = jnp.broadcast_to(src[...], (64, 128))
        even = jnp.sum(jnp.where(lane_c == 2 * row_m, vals, 0.0), 1, keepdims=True)
        odd = jnp.sum(jnp.where(lane_c == 2 * row_m + 1, vals, 0.0), 1, keepdims=True)
        dst[...] = jnp.where(lane_c < half, even, odd)

    to_z(send_r.at[pl.ds(0, nz - 1)], all_r.at[d_me, pl.ds(0, nz - 1)], 0, z).wait_recv()
    for j in range(1, nd):
        peer = lax.rem(d_me + j, nd)
        pltpu.make_async_remote_copy(
            all_r.at[d_me],
            all_r.at[d_me],
            send_sem.at[2],
            recv_sem.at[2],
            device_id={"gx": peer // ng, "gz": lax.rem(peer, ng)},
            device_id_type=MESH,
        ).start()
    to_z(send_l.at[pl.ds(0, nz - 1)], recv_l.at[pl.ds(0, nz - 1)], 1, z).wait_recv()
    to_z(all_r.at[pl.ds(0, nd - 1)], all_r.at[pl.ds(0, nd - 1)], 2, z).wait_recv()

    row_c2 = lax.rem(lax.broadcasted_iota(jnp.int32, (nz * 16, 128), 0) // 8, 2)
    lane64 = lax.broadcasted_iota(jnp.int32, (half, 128), 1)
    for cp in range(2):
        lp = recv_l[:, pl.ds(16 * cp, 16), :].reshape(nz * 16, 128)
        zero = jnp.zeros_like(lp)
        lz = jnp.concatenate(
            [jnp.where(row_c2 == 0, lp, zero), jnp.where(row_c2 == 1, lp, zero)], axis=1
        )
        for d in range(nd):
            rp = all_r[d, :, pl.ds(16 * cp, 16), :].reshape(nz * 16, 128)
            p = jnp.dot(rp.T, lz, preferred_element_type=F32)
            c0, c1 = p[:, 0:128], p[:, 128:256]
            a = jnp.where(lane64 < half, c0[0:64], c1[64:128])
            b = jnp.where(lane64 < half, c1[0:64], c0[64:128])
            tri = (a + pltpu.roll(b, half, 1)).astype(BF16)
            per = rows // cols
            send_t[pl.ds(d * per, per), pl.ds(16 * cp, 16), :] = tri.reshape(per, 16, 128)
    recv_t[z] = send_t[z]
    for j in offsets:
        target = lax.rem(z + j, nz)
        to_z(send_t.at[target], recv_t.at[z], 3, target).start()
    to_z(send_t.at[pl.ds(0, nz - 1)], recv_t.at[pl.ds(0, nz - 1)], 3, z).wait_recv()

    xt = recv_t[...].astype(F32).reshape(nz * 2, 16, 128)
    s = jnp.sum(xt, 0)
    mu = (s + pltpu.roll(s, half, 1)) * (1.0 / 128.0)
    ct = xt - mu
    v = jnp.sum(ct * ct, 0)
    rstd = lax.rsqrt((v + pltpu.roll(v, half, 1)) * (1.0 / 128.0) + 1e-05)
    for m in range(nz * 2):
        y = ct[m] * rstd * gm_buf[pl.ds(m, 1), :] + bm_buf[pl.ds(m, 1), :]
        y_buf[pl.ds(16 * m, 16), :] = y
    for j in range(cols):
        yj = y_buf[pl.ds(j, 64, stride=16), :].astype(BF16)
        p = jnp.dot(yj.T, w2, preferred_element_type=F32)
        o_buf[pl.ds(j, rows, stride=cols), :] = p[0:64, 0:128] + p[64:128, 128:256]
    out_ref[...] = (gate_buf[...] * o_buf[...]).astype(BF16)

    to_z(send_r.at[pl.ds(0, nz - 1)], all_r.at[d_me, pl.ds(0, nz - 1)], 0, z).wait_send()
    to_z(send_l.at[pl.ds(0, nz - 1)], recv_l.at[pl.ds(0, nz - 1)], 1, z).wait_send()
    to_z(all_r.at[pl.ds(0, nd - 1)], all_r.at[pl.ds(0, nd - 1)], 2, z).wait_send()
    to_z(send_t.at[pl.ds(0, nz - 1)], recv_t.at[pl.ds(0, nz - 1)], 3, z).wait_send()


def body(dims, pair, lengths, ln_gain, ln_bias, w_ab, w_gate, out_gain, out_bias, w_out):
    nz, nx, ng, rows, cols = dims
    nd = nx * ng
    flat = rows * cols
    width = pair.shape[2]
    vmem = pl.BlockSpec(memory_space=pltpu.VMEM)
    smem = pl.BlockSpec(memory_space=pltpu.SMEM)
    out = pl.pallas_call(
        functools.partial(kernel, dims),
        out_shape=jax.ShapeDtypeStruct((flat, width), BF16),
        in_specs=[vmem, smem] + [vmem] * 7,
        out_specs=vmem,
        scratch_shapes=[
            pltpu.VMEM((flat, 128), F32),
            pltpu.VMEM((1024, 128), F32),
            pltpu.VMEM((1024, 128), F32),
            pltpu.VMEM((flat, 128), F32),
            pltpu.VMEM((nz, 32, 128), BF16),
            pltpu.VMEM((nz, 32, 128), BF16),
            pltpu.VMEM((nz, 32, 128), BF16),
            pltpu.VMEM((nd, nz, 32, 128), BF16),
            pltpu.VMEM((nz, 32, 128), BF16),
            pltpu.VMEM((nz, 32, 128), BF16),
            pltpu.VMEM((1024, 128), F32),
            pltpu.VMEM((flat, 128), F32),
            pltpu.VMEM((128, 128), F32),
            pltpu.VMEM((64, 128), F32),
            pltpu.VMEM((64, 128), F32),
            pltpu.SemaphoreType.DMA((4,)),
            pltpu.SemaphoreType.DMA((4,)),
        ],
        compiler_params=pltpu.CompilerParams(
            collective_id=0, has_side_effects=True, vmem_limit_bytes=48 * 2**20
        ),
    )(
        pair.reshape(flat, width),
        lengths,
        ln_gain.reshape(1, -1),
        ln_bias.reshape(1, -1),
        w_ab,
        w_gate,
        out_gain.reshape(1, -1),
        out_bias.reshape(1, -1),
        w_out,
    )
    return out.reshape(pair.shape)


def solution(mesh):
    in_specs = (P(("grp", "gx", "gz"), "gy", None), P("grp"), P(), P(), P(), P(), P(), P(), P())
    out_specs = P(("grp", "gx", "gz"), "gy", None)

    def whole(pair, *rest):
        nz, nx, ng = mesh.shape["gy"], mesh.shape["gx"], mesh.shape["gz"]
        rows = pair.shape[0] // (mesh.shape["grp"] * nx * ng)
        cols = pair.shape[1] // nz
        dims = (nz, nx, ng, rows, cols)
        fn = jax.shard_map(
            functools.partial(body, dims),
            mesh=mesh,
            in_specs=in_specs,
            out_specs=out_specs,
            check_vma=False,
        )
        return fn(pair, *rest)

    return whole
```

time: 455 us -> 135 us (0.30)
  the two profiles are of different devices: /device:TPU:36 before, /device:TPU:38 now
where the time goes in v1:
time: 135 us; the launch traced here: 134 us
  Pallas kernels  129 us (96%)
  local copies, waits for them, and re-layouts  4.74 us (4%)
    pallas_call x1, Pallas kernels, body(): pl.pallas_call(functools.partial(kernel, dims), out_shape=jax.ShapeDtypeS...  129 us
    unnamed x17, local copies, waits for them, and re-layouts  4.74 us

profile of v1, /device:TPU:38, one launch (start us, length us, event | category | flops | bytes accessed | tf_op | source)
XLA Modules:
  0.0 134.3 jit_solution(11112623382089898181)
XLA Ops:
  0.7 0.0 copy-start.7
  0.7 0.0 copy-start.4
  0.7 0.0 copy-start.5
  0.7 0.0 copy-start.6
  0.7 0.6 copy-done.7
  1.3 0.0 copy-done.4
  1.3 0.0 copy-done.5
  1.3 0.0 copy-done.6
  1.4 0.0 copy-start
  1.4 0.9 copy-done
  2.3 0.0 copy-start.1
  2.3 0.9 copy-done.1
  3.2 0.0 copy-start.2
  3.2 0.8 copy-done.2
  4.0 0.0 copy-start.3
  4.0 0.8 copy-done.3
  4.7 128.9 %shard_map.91 = bf16[1024,128]{1,0:T(8,128)(2,1)S(1)} custom-call(bf16[1024,128]{1,0:T(8,128)(2,1)S(1)} %bitcast.7, s32[1]{0:T(128)S(6)} %copy.11.len_ref, f32[1,128]{1,0:T(1,128)S(1)} %bitcast.8, f32[1,128]{1,0:T(1,128)S(1)} %bitcast.9, bf16[128,512]{1,0:T(8,128)(2,1)S(1)} %copy-done.1, bf16[128,128]{1,0:T(8,128)(2,1)S(1)} %copy-done.2, ...), custom_call_target="tpu_custom_call" | custom-call | tf_op jit(solution)/shard_map/pallas_call | solution.py:198
  133.6 0.7 copy.12
Async XLA Ops:
  0.7 0.7 copy-start.7
  0.7 0.7 copy-start.4
  0.7 0.7 copy-start.5
  0.7 0.7 copy-start.6
  1.4 0.9 copy-start
  2.3 0.9 copy-start.1
  3.2 0.8 copy-start.2
  4.0 0.8 copy-start.3

commit v2 on v0

v2 whole, which is shorter than its diff:
```python
import functools

import jax
import jax.numpy as jnp
from jax import lax
from jax.experimental import pallas as pl
from jax.experimental.pallas import tpu as pltpu
from jax.sharding import PartitionSpec as P

MESH = pl.DeviceIdType.MESH
F32 = jnp.float32
BF16 = jnp.bfloat16


def kernel(
    dims,
    pair_hbm,
    len_ref,
    ln_gain_hbm,
    ln_bias_hbm,
    w_ab_hbm,
    w_gate_hbm,
    out_gain_hbm,
    out_bias_hbm,
    w_out_hbm,
    out_ref,
    pair_ref,
    ln_gain_ref,
    ln_bias_ref,
    out_gain_ref,
    out_bias_ref,
    w_ab_ref,
    w_gate_ref,
    w_out_ref,
    load_sem,
    norm_f32,
    buf,
    gate_buf,
    send_lr,
    all_lr,
    send_t,
    recv_t,
    y_buf,
    o_buf,
    send_sem,
    lr_sem,
    core_sem,
    t_sem,
    chain_sem,
    near_sem,
    in_sem,
):
    nz, nx, ng, rows, cols = dims
    nd = nx * ng
    owners = nz * nx
    z = lax.axis_index("gy")
    x = lax.axis_index("gx")
    g = lax.axis_index("gz")
    d_me = x * ng + g
    length = len_ref[0]
    q = lax.rem(z + nz - 1, nz)

    def z_of(place):
        return lax.rem(place + 1, nz)

    def signal(sem, target):
        pl.semaphore_signal(sem, inc=1, device_id=target, device_id_type=MESH)

    def remote(src, dst, k, sem, target):
        return pltpu.make_async_remote_copy(
            src, dst, send_sem.at[k], sem, device_id=target, device_id_type=MESH
        )

    offsets = []
    for j in range(nz // 2, 0, -1):
        offsets.append(j)
        if 2 * j != nz:
            offsets.append(nz - j)

    loads = [
        pltpu.make_async_copy(src, dst, load_sem.at[k])
        for k, (src, dst) in enumerate(
            (
                (pair_hbm, pair_ref),
                (w_ab_hbm, w_ab_ref),
                (w_gate_hbm, w_gate_ref),
                (w_out_hbm, w_out_ref),
                (ln_gain_hbm, ln_gain_ref),
                (ln_bias_hbm, ln_bias_ref),
                (out_gain_hbm, out_gain_ref),
                (out_bias_hbm, out_bias_ref),
            )
        )
    ]
    for load in loads:
        load.start()

    barrier = pltpu.get_barrier_semaphore()
    expect = nd - 1
    for step in (-2, -1, 1, 2):
        there = jnp.logical_and(q + step >= 0, q + step < nz)
        expect = expect + jnp.where(there, 1, 0)

        @pl.when(there)
        def _(step=step):
            signal(barrier, {"gy": z_of(q + step)})

    for j in range(1, nd):
        peer = lax.rem(d_me + j, nd)
        signal(barrier, {"gx": peer // ng, "gz": lax.rem(peer, ng)})
    loads[0].wait()
    loads[4].wait()
    loads[5].wait()
    xs = pair_ref[...].astype(F32)
    mean = jnp.mean(xs, -1, keepdims=True)
    cen = xs - mean
    var = jnp.mean(cen * cen, -1, keepdims=True)
    normed = (cen * lax.rsqrt(var + 1e-05) * ln_gain_ref[...] + ln_bias_ref[...]).astype(BF16)
    norm_f32[...] = normed.astype(F32)

    pl.semaphore_wait(barrier, expect)

    @pl.when(q < nz - 1)
    def _():
        signal(near_sem, {"gy": z_of(q + 1)})

    @pl.when(q >= 1)
    def _():
        pl.semaphore_wait(near_sem, 1)

    @pl.when(q >= 2)
    def _():
        pl.semaphore_wait(chain_sem, 1)

    @pl.when(q < nz - 2)
    def _():
        signal(chain_sem, {"gy": z_of(q + 2)})

    for j in offsets:
        other = lax.rem(q + j, nz)

        @pl.when(other < q)
        def _(other=other):
            signal(in_sem.at[q], {"gy": z_of(other)})

    loads[1].wait()
    w_t = w_ab_ref[...].T
    lane = lax.broadcasted_iota(jnp.int32, (1, 128), 1)
    row_live = (d_me * rows + lax.rem(lane, rows)) < length
    low = lax.broadcasted_iota(jnp.int32, (128, 128), 1) < rows
    for k in range(cols):
        n_k = norm_f32[pl.ds(k, rows, stride=cols), :]
        n_k = jnp.concatenate([n_k, n_k], axis=0).astype(BF16)
        proj = lax.dot_general(
            w_t, n_k, (((1,), (1,)), ((), ())), preferred_element_type=F32
        )
        mask = jnp.where(jnp.logical_and(row_live, z * cols + k < length), 1.0, 0.0)
        gate = jnp.where(low, proj[0:128], proj[256:384])
        value = jnp.where(low, proj[128:256], proj[384:512])
        buf[pl.ds(k, 128, stride=cols), :] = mask * jax.nn.sigmoid(gate) * value
    send_lr[...] = buf[...].astype(BF16).reshape(send_lr.shape)

    def send_to(place):
        for j in range(nx):
            xt = lax.rem(x + j, nx)
            remote(
                send_lr.at[z_of(place) * nx + xt],
                all_lr.at[g, x, q],
                0,
                lr_sem.at[q],
                {"gy": z_of(place), "gx": xt},
            ).start()

    for j in offsets:
        other = lax.rem(q + j, nz)

        @pl.when(other < q)
        def _(other=other):
            send_to(other)

    for j in range(1, nx):
        xt = lax.rem(x + j, nx)
        remote(
            send_lr.at[z * nx + xt], all_lr.at[g, x, q], 0, lr_sem.at[q], {"gx": xt}
        ).start()
    all_lr[g, x, q] = send_lr[z * nx + x]

    @pl.loop(q + 1, nz)
    def _(other):
        pl.semaphore_wait(in_sem.at[other], 1)
        send_to(other)

    loads[2].wait()
    gate_buf[...] = jax.nn.sigmoid(
        jnp.dot(norm_f32[...].astype(BF16), w_gate_ref[...], preferred_element_type=F32)
    )

    partner = {"gz": lax.rem(g + 1, ng)}
    per_group = 4
    for grp in range(nz // per_group):
        for s in range(grp * per_group, (grp + 1) * per_group):

            @pl.when(s != q)
            def _(s=s):
                part = all_lr.at[0, :, s]
                remote(part, part, 0, lr_sem.at[s], partner).wait_recv()

            @pl.when(s == q)
            def _(s=s):
                part = all_lr.at[0, pl.ds(0, nx - 1), s]
                remote(part, part, 0, lr_sem.at[s], partner).wait_recv()

        part = all_lr.at[g, :, pl.ds(grp * per_group, per_group)]
        remote(part, part, 1, core_sem, partner).start()
    remote(all_lr.at[0], all_lr.at[0], 1, core_sem, partner).wait_recv()

    right = []
    for d in range(nd):
        block = all_lr[d % ng, d // ng].reshape(nz * cols, 128)
        right.append(block.T[rows : 2 * rows])
    right = jnp.concatenate(right, axis=0)
    low8 = lax.broadcasted_iota(jnp.int32, (nz, 8, 128), 2) < rows
    for xt in range(nx):
        left = all_lr[g, xt].reshape(nz * cols, 128)
        tri = jnp.dot(right, left, preferred_element_type=F32).reshape(nz, 16, 128)
        turned = pltpu.roll(tri[:, 8:16].reshape(nz * 8, 128), rows, 1).reshape(nz, 8, 128)
        send_t[:, xt] = jnp.where(low8, tri[:, 0:8], turned).astype(BF16)

    for zt in range(nz):
        for j in range(nx):
            xt = lax.rem(x + j, nx)
            if j == 0:

                @pl.when(z != zt)
                def _(zt=zt, xt=xt):
                    remote(
                        send_t.at[zt, xt], recv_t.at[z * nx + x], 2, t_sem, {"gy": zt, "gx": xt}
                    ).start()
            else:
                remote(
                    send_t.at[zt, xt], recv_t.at[z * nx + x], 2, t_sem, {"gy": zt, "gx": xt}
                ).start()
    recv_t[z * nx + x] = send_t[z, x]

    others = recv_t.at[pl.ds(0, owners - 1)]
    remote(others, others, 2, t_sem, partner).wait_recv()

    for k in (3, 6, 7):
        loads[k].wait()
    ct = recv_t[...].astype(F32)
    ct = ct - jnp.sum(ct, 0) * (1.0 / owners)
    rstd = lax.rsqrt(jnp.sum(ct * ct, 0) * (1.0 / owners) + 1e-05)
    for c in range(owners):
        y_buf[pl.ds(8 * c, 8), :] = ct[c] * rstd * out_gain_ref[c] + out_bias_ref[c]
    w_out = w_out_ref[...]
    for j in range(8):
        yj = y_buf[pl.ds(j, owners, stride=8), :].astype(BF16)
        p = jnp.dot(yj.T, w_out, preferred_element_type=F32)
        o_buf[pl.ds(j, rows, stride=cols), :] = p[0:rows]
        o_buf[pl.ds(8 + j, rows, stride=cols), :] = p[rows : 2 * rows]
    out_ref[...] = (gate_buf[...] * o_buf[...]).astype(BF16)

    part = send_lr.at[pl.ds(0, owners - 1)]
    remote(part, part, 0, t_sem, partner).wait_send()
    remote(all_lr.at[0], all_lr.at[0], 1, t_sem, partner).wait_send()
    remote(others, others, 2, t_sem, partner).wait_send()


def body(dims, pair, lengths, ln_gain, ln_bias, w_ab, w_gate, out_gain, out_bias, w_out):
    nz, nx, ng, rows, cols = dims
    flat = rows * cols
    width = pair.shape[2]
    vmem = pl.BlockSpec(memory_space=pltpu.VMEM)
    hbm = pl.BlockSpec(memory_space=pltpu.HBM)
    smem = pl.BlockSpec(memory_space=pltpu.SMEM)
    out = pl.pallas_call(
        functools.partial(kernel, dims),
        out_shape=jax.ShapeDtypeStruct((flat, width), BF16),
        in_specs=[hbm, smem] + [hbm] * 7,
        out_specs=vmem,
        scratch_shapes=[
            pltpu.VMEM((flat, width), BF16),
            pltpu.VMEM((1, width), F32),
            pltpu.VMEM((1, width), F32),
            pltpu.SMEM((nz * nx,), F32),
            pltpu.SMEM((nz * nx,), F32),
            pltpu.VMEM(w_ab.shape, BF16),
            pltpu.VMEM(w_gate.shape, BF16),
            pltpu.VMEM(w_out.shape, BF16),
            pltpu.SemaphoreType.DMA((8,)),
            pltpu.VMEM((flat, 128), F32),
            pltpu.VMEM((128 * cols, 128), F32),
            pltpu.VMEM((flat, 128), F32),
            pltpu.VMEM((nz * nx, cols, 128), BF16),
            pltpu.VMEM((ng, nx, nz, cols, 128), BF16),
            pltpu.VMEM((nz, nx, 8, 128), BF16),
            pltpu.VMEM((nz * nx, 8, 128), BF16),
            pltpu.VMEM((nz * nx * 8, 128), F32),
            pltpu.VMEM((flat, 128), F32),
            pltpu.SemaphoreType.DMA((3,)),
            pltpu.SemaphoreType.DMA((nz,)),
            pltpu.SemaphoreType.DMA,
            pltpu.SemaphoreType.DMA,
            pltpu.SemaphoreType.REGULAR,
            pltpu.SemaphoreType.REGULAR,
            pltpu.SemaphoreType.REGULAR((nz,)),
        ],
        compiler_params=pltpu.CompilerParams(
            collective_id=0, has_side_effects=True, vmem_limit_bytes=60 * 1024 * 2**10
        ),
    )(
        pair.reshape(flat, width),
        lengths,
        ln_gain.reshape(1, -1),
        ln_bias.reshape(1, -1),
        w_ab,
        w_gate,
        out_gain,
        out_bias,
        w_out,
    )
    return out.reshape(pair.shape)


def solution(mesh):
    in_specs = (P(("grp", "gx", "gz"), "gy", None), P("grp"), P(), P(), P(), P(), P(), P(), P())
    out_specs = P(("grp", "gx", "gz"), "gy", None)

    def whole(pair, *rest):
        nz, nx, ng = mesh.shape["gy"], mesh.shape["gx"], mesh.shape["gz"]
        rows = pair.shape[0] // (mesh.shape["grp"] * nx * ng)
        cols = pair.shape[1] // nz
        dims = (nz, nx, ng, rows, cols)
        fn = jax.shard_map(
            functools.partial(body, dims),
            mesh=mesh,
            in_specs=in_specs,
            out_specs=out_specs,
            check_vma=False,
        )
        return fn(pair, *rest)

    return whole
```

time: 455 us -> 124 us (0.27)
  the two profiles are of different devices: /device:TPU:36 before, /device:TPU:233 now
where the time goes in v2:
time: 124 us
  Pallas kernels  121 us (98%)
  local copies, waits for them, and re-layouts  1.67 us (1%)
    pallas_call x1, Pallas kernels, body(): pl.pallas_call(functools.partial(kernel, dims), out_shape=jax.ShapeDtypeS...  121 us

profile of v2, /device:TPU:233, one launch (start us, length us, event | category | flops | bytes accessed | tf_op | source)
XLA Modules:
  0.0 123.6 jit_solution(17635348112243050896)
XLA Ops:
  0.7 121.3 %shard_map.91 = bf16[1024,128]{1,0:T(8,128)(2,1)} custom-call(bf16[1024,128]{1,0:T(8,128)(2,1)} %bitcast.5, s32[1]{0:T(128)S(6)} %copy.11.len_ref, f32[1,128]{1,0:T(1,128)} %bitcast.6, f32[1,128]{1,0:T(1,128)} %bitcast.7, bf16[128,512]{1,0:T(8,128)(2,1)} %w_ab_hbm.1, bf16[128,128]{1,0:T(8,128)(2,1)} %w_gate_hbm.1, f32[128]{0:T(128)} %out_gain_hbm.1, ...), custom_call_target="tpu_custom_call" | custom-call | tf_op jit(solution)/shard_map/pallas_call | solution.py:276
  122.0 1.7 %copy.12 = bf16[64,16,128]{2,1,0:T(8,128)(2,1)} copy(bf16[64,16,128]{2,1,0:T(8,128)(2,1)} %bitcast.4) | data formatting | bytes 524288

commit v3 on v2

--- a/solution.py
+++ b/solution.py
@@ -226,7 +226,7 @@
         turned = pltpu.roll(tri[:, 8:16].reshape(nz * 8, 128), rows, 1).reshape(nz, 8, 128)
         send_t[:, xt] = jnp.where(low8, tri[:, 0:8], turned).astype(BF16)
 
-    for zt in range(nz):
+    for zt in [k // 2 + (k % 2) * (nz // 2) for k in range(nz)]:
         for j in range(nx):
             xt = lax.rem(x + j, nx)
             if j == 0:
@@ -273,6 +273,9 @@
     vmem = pl.BlockSpec(memory_space=pltpu.VMEM)
     hbm = pl.BlockSpec(memory_space=pltpu.HBM)
     smem = pl.BlockSpec(memory_space=pltpu.SMEM)
+    def stay(a):
+        return pltpu.with_memory_space_constraint(a, pltpu.HBM)
+
     out = pl.pallas_call(
         functools.partial(kernel, dims),
         out_shape=jax.ShapeDtypeStruct((flat, width), BF16),
@@ -306,18 +309,18 @@
             pltpu.SemaphoreType.REGULAR((nz,)),
         ],
         compiler_params=pltpu.CompilerParams(
-            collective_id=0, has_side_effects=True, vmem_limit_bytes=60 * 1024 * 2**10
+            collective_id=0, has_side_effects=True, vmem_limit_bytes=48 * 2**20
         ),
     )(
-        pair.reshape(flat, width),
+        stay(pair.reshape(flat, width)),
         lengths,
-        ln_gain.reshape(1, -1),
-        ln_bias.reshape(1, -1),
-        w_ab,
-        w_gate,
-        out_gain,
-        out_bias,
-        w_out,
+        stay(ln_gain.reshape(1, -1)),
+        stay(ln_bias.reshape(1, -1)),
+        stay(w_ab),
+        stay(w_gate),
+        stay(out_gain),
+        stay(out_bias),
+        stay(w_out),
     )
     return out.reshape(pair.shape)
 

time: 124 us -> 120 us (0.968)
  the two profiles are of different devices: /device:TPU:233 before, /device:TPU:161 now
where the time goes in v3:
time: 120 us; the launch traced here: 119 us
  Pallas kernels  118 us (98%)
    pallas_call x1, Pallas kernels, body(): pl.pallas_call(functools.partial(kernel, dims), out_shape=jax.ShapeDtypeS...  118 us

profile of v3, /device:TPU:161, one launch (start us, length us, event | category | flops | bytes accessed | tf_op | source)
XLA Modules:
  0.0 119.5 jit_solution(5917734524140581493)
XLA Ops:
  0.7 118.1 %shard_map.91 = bf16[1024,128]{1,0:T(8,128)(2,1)S(1)} custom-call(bf16[1024,128]{1,0:T(8,128)(2,1)} %bitcast.5, s32[1]{0:T(128)S(6)} %copy.11.len_ref, f32[1,128]{1,0:T(1,128)} %bitcast.6, f32[1,128]{1,0:T(1,128)} %bitcast.7, bf16[128,512]{1,0:T(8,128)(2,1)} %w_ab_hbm.1, bf16[128,128]{1,0:T(8,128)(2,1)} %w_gate_hbm.1, f32[128]{0:T(128)} %out_gain_hbm.1, ...), custom_call_target="tpu_custom_call" | custom-call | tf_op jit(solution)/shard_map/pallas_call | solution.py:279
  118.8 0.7 copy.12

commit v4 on v3

--- a/solution.py
+++ b/solution.py
@@ -118,31 +118,6 @@
     normed = (cen * lax.rsqrt(var + 1e-05) * ln_gain_ref[...] + ln_bias_ref[...]).astype(BF16)
     norm_f32[...] = normed.astype(F32)
 
-    pl.semaphore_wait(barrier, expect)
-
-    @pl.when(q < nz - 1)
-    def _():
-        signal(near_sem, {"gy": z_of(q + 1)})
-
-    @pl.when(q >= 1)
-    def _():
-        pl.semaphore_wait(near_sem, 1)
-
-    @pl.when(q >= 2)
-    def _():
-        pl.semaphore_wait(chain_sem, 1)
-
-    @pl.when(q < nz - 2)
-    def _():
-        signal(chain_sem, {"gy": z_of(q + 2)})
-
-    for j in offsets:
-        other = lax.rem(q + j, nz)
-
-        @pl.when(other < q)
-        def _(other=other):
-            signal(in_sem.at[q], {"gy": z_of(other)})
-
     loads[1].wait()
     w_t = w_ab_ref[...].T
     lane = lax.broadcasted_iota(jnp.int32, (1, 128), 1)
@@ -159,6 +134,31 @@
         value = jnp.where(low, proj[128:256], proj[384:512])
         buf[pl.ds(k, 128, stride=cols), :] = mask * jax.nn.sigmoid(gate) * value
     send_lr[...] = buf[...].astype(BF16).reshape(send_lr.shape)
+
+    pl.semaphore_wait(barrier, expect)
+
+    @pl.when(q < nz - 1)
+    def _():
+        signal(near_sem, {"gy": z_of(q + 1)})
+
+    @pl.when(q >= 1)
+    def _():
+        pl.semaphore_wait(near_sem, 1)
+
+    @pl.when(q >= 2)
+    def _():
+        pl.semaphore_wait(chain_sem, 1)
+
+    @pl.when(q < nz - 2)
+    def _():
+        signal(chain_sem, {"gy": z_of(q + 2)})
+
+    for j in offsets:
+        other = lax.rem(q + j, nz)
+
+        @pl.when(other < q)
+        def _(other=other):
+            signal(in_sem.at[q], {"gy": z_of(other)})
 
     def send_to(place):
         for j in range(nx):

time: 120 us -> 120 us (level)
  no operation moved by 1% of the time
where the time goes in v4:
time: 120 us
  Pallas kernels  118 us (98%)
    pallas_call x1, Pallas kernels, body(): pl.pallas_call(functools.partial(kernel, dims), out_shape=jax.ShapeDtypeS...  118 us

profile of v4, /device:TPU:161, one launch (start us, length us, event | category | flops | bytes accessed | tf_op | source)
XLA Modules:
  0.0 119.7 jit_solution(7203584495513457579)
XLA Ops:
  0.7 118.4 %shard_map.91 = bf16[1024,128]{1,0:T(8,128)(2,1)S(1)} custom-call(bf16[1024,128]{1,0:T(8,128)(2,1)} %bitcast.5, s32[1]{0:T(128)S(6)} %copy.11.len_ref, f32[1,128]{1,0:T(1,128)} %bitcast.6, f32[1,128]{1,0:T(1,128)} %bitcast.7, bf16[128,512]{1,0:T(8,128)(2,1)} %w_ab_hbm.1, bf16[128,128]{1,0:T(8,128)(2,1)} %w_gate_hbm.1, f32[128]{0:T(128)} %out_gain_hbm.1, ...), custom_call_target="tpu_custom_call" | custom-call | tf_op jit(solution)/shard_map/pallas_call | solution.py:279
  119.0 0.7 copy.12
